TPU v7x, 32 devices: a whole 2x2x4 slice. The times are simulated.
32 devices in a mesh: zero: 8 (over z, x), model: 4 (over y, core).
Axes of the slice: x: 2, y: 2, z: 4, core: 2. Of those that a mesh axis runs over, the one named last changes fastest.
Arguments:
- train_up: bfloat16 [12288, 49152], P('zero', 'model'), may hold values from -0.078125 to 0.078125
- low_up: bfloat16 [12288, 32], P('zero'), may hold values from -0.0546875 to 0.0546875
- high_up: bfloat16 [32, 49152], P(None, 'model'), may hold values from -1 to 1
- norm_train: float32 [12288], P(('zero', 'model')), may hold values from 0.25 to 1.75
- norm_step: float32 [12288], P(('zero', 'model')), may hold values from -0.3 to 0.3
Outputs:
- serving_up: bfloat16 [12288, 49152], P(None, ('model', 'zero'))
- scale_up: float32 [49152], P(('model', 'zero'))
- serve_norm: bfloat16 [12288], replicated
All inputs are finite; a program needn't handle non-finite values. Where the computation divides by a largest or mean magnitude, that divisor is 1e-20 or more.
Results may differ from a plain program's by a relative error of at most 0.001.
Values may be sent and summed in bfloat16 or wider, within the bound.
No kernel may reach another device: no remote copies, remote signals or barrier semaphores. Data moves between devices by JAX's collectives and lax.ppermute only.
A program may use at most 192 MiB of HBM per device.

v0:
```python
import jax
import jax.numpy as jnp
from jax import lax
from jax.sharding import PartitionSpec as P

D_MODEL = 12288


mix_rate = 0.5


def local(train_up, low_up, high_up, norm_train, norm_step):
    whole_up = train_up.astype(jnp.float32) + mix_rate * jnp.dot(
        low_up, high_up, preferred_element_type=jnp.float32
    )
    total_up = lax.psum(jnp.sum(jnp.abs(whole_up), axis=0), "zero")
    scale_up = total_up / D_MODEL
    narrow_up = (whole_up / scale_up).astype(jnp.bfloat16)
    serving_up = lax.all_to_all(narrow_up, "zero", split_axis=1, concat_axis=0, tiled=True)
    place = lax.axis_index("zero")
    scale_up = lax.dynamic_slice_in_dim(scale_up, place * serving_up.shape[1], serving_up.shape[1])
    serve_norm = lax.all_gather(
        (norm_train + norm_step).astype(jnp.bfloat16), ("zero", "model"), axis=0, tiled=True
    )
    return (serving_up, scale_up, serve_norm)


def solution(mesh):
    in_specs = (
        P("zero", "model"),
        P("zero", None),
        P(None, "model"),
        P(("zero", "model")),
        P(("zero", "model")),
    )
    out_specs = (P(None, ("model", "zero")), P(("model", "zero")), P())
    return jax.shard_map(local, mesh=mesh, in_specs=in_specs, out_specs=out_specs, check_vma=False)
```

profile of v0, /device:TPU:17, one launch (start us, length us, event | category | flops | bytes accessed | tf_op | source)
XLA Modules:
  0.0 1004.6 jit_solution(341893430353904681)
XLA Ops:
  0.6 0.0 copy-start
  0.6 1.1 copy-done
  1.8 38.0 %abs_reduce_fusion = (f32[12288]{0:T(1024)S(1)}, f32[1536,12288]{1,0:T(8,128)}) fusion(bf16[1536,32]{0,1:T(8,128)(2,1)} %param.6, bf16[32,12288]{1,0:T(8,128)(2,1)S(1)} %copy-done, bf16[1536,12288]{1,0:T(8,128)(2,1)} %param.5), kind=kOutput, calls=%fused_computation.1 | convolution fusion | flops 1302319104 | bytes 114180096 | tf_op jit(solution)/shard_map/dot_general | solution.py:13
  39.8 25.9 %psum.7 = f32[12288]{0:T(1024)S(1)} all-reduce(f32[12288]{0:T(1024)S(1)} %get-tuple-element.3), channel_id=1, replica_groups=mesh['zero'=8,'model'=4] {'zero'}, use_global_device_ids=true, to_apply=%region_1.0 | all-reduce | flops 12288 | bytes 98304 | tf_op jit(solution)/shard_map/psum | solution.py:16
  65.7 36.5 %divide_convert_fusion = bf16[1536,12288]{1,0:T(8,128)(2,1)} fusion(f32[1536,12288]{1,0:T(8,128)} %get-tuple-element.4, f32[12288]{0:T(1024)S(1)} %broadcast_multiply_fusion), kind=kLoop, calls=%fused_computation | loop fusion | flops 37748736 | bytes 113295360 | tf_op jit(solution)/shard_map/convert_element_type | solution.py:18
  102.2 0.0 copy-start.2
  102.2 0.0 copy-start.3
  102.2 26.0 %copy.13 = bf16[192,8,8,1536]{3,2,0,1:T(8,128)(2,1)} copy(bf16[192,8,8,1536]{3,2,1,0:T(8,128)(2,1)} %bitcast.10) | data formatting | bytes 75497472 | tf_op jit(solution)/shard_map/all_to_all | solution.py:19
  128.2 0.0 copy-start.1
  128.2 12.3 %all-to-all-start = ((bf16[1536,8,1536]{2,0,1:T(8,128)(2,1)}), bf16[1536,8,1536]{2,0,1:T(8,128)(2,1)}, u32[]{:S(2)}, u32[]{:S(2)}) async-start(bf16[1536,8,1536]{2,0,1:T(8,128)(2,1)} %bitcast.9), calls=%async_computation | async-start | bytes 75497472 | tf_op jit(solution)/shard_map/all_to_all | solution.py:19
  140.5 0.7 dynamic_slice.3
  141.1 0.0 copy-done.2
  141.1 0.0 copy-done.3
  141.2 836.7 %all-gather = bf16[32,1,384]{2,1,0:T(2,128)(2,1)S(1)} all-gather(bf16[1,1,384]{2,1,0:T(2,128)(2,1)S(1)} %reshape.10), channel_id=1, replica_groups=mesh['zero'=8,'model'=4] {'zero','model'}, dimensions={0}, use_global_device_ids=true | all-gather | bytes 25344 | tf_op jit(solution)/shard_map/all_gather | solution.py:22
  977.9 0.1 reduce
  978.0 0.6 reshape.11
  978.7 0.0 all-to-all-done
  978.7 25.9 %copy.15 = bf16[12288,1536]{1,0:T(8,128)(2,1)} copy(bf16[12288,1536]{1,0:T(8,128)(2,1)} %bitcast.1) | data formatting | bytes 75497472
  1004.6 0.0 copy-done.1
  (3 shorter events, 0.0 us)
Async XLA Ops:
  0.6 1.1 copy-start
  102.2 38.9 %copy-start.2 = (f32[384]{0:T(512)S(1)}, f32[384]{0:T(512)}, u32[]{:S(2)}) copy-start(f32[384]{0:T(512)} %param.8) | copy-start | bytes 4612
  102.2 38.9 %copy-start.3 = (f32[384]{0:T(512)S(1)}, f32[384]{0:T(512)}, u32[]{:S(2)}) copy-start(f32[384]{0:T(512)} %param.9) | copy-start | bytes 4612
  128.2 876.4 %copy-start.1 = (bf16[32,12288]{1,0:T(8,128)(2,1)S(1)}, bf16[32,12288]{1,0:T(8,128)(2,1)}, u32[]{:S(2)}) copy-start(bf16[32,12288]{1,0:T(8,128)(2,1)} %param.7) | copy-start | bytes 2359300
  128.2 850.5 %all-to-all-start = ((bf16[1536,8,1536]{2,0,1:T(8,128)(2,1)}), bf16[1536,8,1536]{2,0,1:T(8,128)(2,1)}, u32[]{:S(2)}, u32[]{:S(2)}) async-start(bf16[1536,8,1536]{2,0,1:T(8,128)(2,1)} %bitcast.9), calls=%async_computation | async-start | bytes 75497472 | tf_op jit(solution)/shard_map/all_to_all | solution.py:19
where the time goes:
time: 1000 us
  blocking collectives  863 us (86%)
  local copies, waits for them, and re-layouts  54.3 us (5%)
  matrix products  38 us (4%)
  other arithmetic  36.6 us (4%)
  starting transfers between devices  12.3 us (1%)
    all_gather x1, blocking collectives, local(): lax.all_gather((norm_train + norm_step).astype(jnp.bfloat16), ('zero', 'm...  837 us
    dot_general x1, matrix products, local(): jnp.dot(low_up, high_up, preferred_element_type=jnp.float32)  38 us
    convert_element_type x1, other arithmetic, local(): narrow_up = (whole_up / scale_up).astype(jnp.bfloat16)  36.5 us
    unnamed x11, local copies, waits for them, and re-layouts  27.7 us
    all_to_all x1, local copies, waits for them, and re-layouts, local(): lax.all_to_all(narrow_up, 'zero', split_axis=1, concat_axis=0, tiled=True)  26 us
    psum x1, blocking collectives, local(): total_up = lax.psum(jnp.sum(jnp.abs(whole_up), axis=0), 'zero')  25.9 us
  transfers between devices with their start and end apart: 1, of which 0 were waited for; matrix products, arithmetic and copies ran while one was open for 0% of the time, Pallas kernels for 0%

commit v1 on v0

v1 whole, which is shorter than its diff:
```python
import functools

import jax
import jax.numpy as jnp
from jax import lax
from jax.experimental import pallas as pl
from jax.experimental.pallas import tpu as pltpu
from jax.sharding import PartitionSpec as P


mix_rate = 0.5


def partner_pairs(size, step):
    if size & (size - 1) == 0:
        return [(s, s ^ step) for s in range(size)]
    return [(s, (s + step) % size) for s in range(size)]


def target_of(me, size, step):
    if size & (size - 1) == 0:
        return me ^ step
    return lax.rem(me + step, size)


def source_of(me, size, step):
    if size & (size - 1) == 0:
        return me ^ step
    return lax.rem(me + size - step, size)


def steps_of(zero):
    return list(range(zero // 2, zero)), list(range(1, zero // 2))


def pieces_of(zero, rows):
    far, near = steps_of(zero)
    fourth = rows // 4
    pieces = {k: [(0, rows)] for k in far + near}
    pieces[far[-1]] = [(0, 2 * fourth), (2 * fourth, fourth), (3 * fourth, fourth)]
    pieces[far[0]] = [(0, fourth), (fourth, 3 * fourth)]
    return pieces


def merge_body(place_ref, block_ref, low_ref, high_ref, inverse_ref, *rest):
    out_ref = rest[-1]
    whole = block_ref[...].astype(jnp.float32) + mix_rate * jnp.dot(
        low_ref[...], high_ref[...], preferred_element_type=jnp.float32
    )
    out_ref[...] = (whole * inverse_ref[...]).astype(out_ref.dtype)


def merge_block(out, total_rows, block, low, high, inverse, place, in_column, full, start):
    width = high.shape[1]
    rows = block.shape[0]
    tile = full // 4
    while tile * width * 2 > 1 << 20 and tile % 32 == 0:
        tile //= 2
    steps = rows // tile
    per_place = full // tile
    first = start // tile
    specs = [
        pl.BlockSpec((tile, width), lambda i, p: (i, p[1])),
        pl.BlockSpec((tile, low.shape[1]), lambda i, p: (p[0] * per_place + first + i, 0)),
        pl.BlockSpec((low.shape[1], width), lambda i, p: (0, 0)),
        pl.BlockSpec((1, width), lambda i, p: (0, 0)),
    ]
    operands = [block, low, high, inverse]
    aliases = {}
    if out is not None:
        specs.append(pl.BlockSpec(memory_space=pl.ANY))
        operands.append(out)
        aliases = {5: 0}
    place = jnp.stack([place, in_column]).astype(jnp.int32)
    return pl.pallas_call(
        merge_body,
        grid_spec=pltpu.PrefetchScalarGridSpec(
            num_scalar_prefetch=1,
            grid=(steps,),
            in_specs=specs,
            out_specs=pl.BlockSpec((tile, width), lambda i, p: (p[0] * per_place + first + i, 0)),
        ),
        out_shape=jax.ShapeDtypeStruct((total_rows, width), jnp.bfloat16),
        input_output_aliases=aliases,
        compiler_params=pltpu.CompilerParams(vmem_limit_bytes=24 << 20),
        cost_estimate=pl.CostEstimate(
            flops=2 * rows * width * low.shape[1], bytes_accessed=4 * rows * width, transcendentals=0
        ),
    )(place, *operands)


def local(zero, model, *arguments):
    return share(zero, model, *arguments)


def share(zero, model, train_up, low_up, high_up, norm_train, norm_step):
    rows, columns = train_up.shape
    rank = low_up.shape[1]
    width = columns // zero
    quarter = rows // model
    total_rows = rows * zero
    me = lax.axis_index("zero")
    mine = lax.axis_index("model")

    far, near = steps_of(zero)
    order = far + near

    def send(value, k, axis, size):
        return lax.ppermute(value, axis, partner_pairs(size, k))

    def after(value, *others):
        return lax.optimization_barrier((value, *others))[0]

    def cut(source, k, start, count):
        return lax.dynamic_slice(source, (start, target_of(me, zero, k) * width), (count, width))

    def send_block(piece, k):
        return send(piece, k, "zero", zero)

    def send_small(value, k):
        return send(value, k, "zero", zero)

    pieces = pieces_of(zero, rows)
    blocks = {}

    gate = train_up
    for start, count in pieces[far[0]]:
        piece = cut(gate, far[0], start, count)
        blocks[far[0], start] = send_block(piece, far[0])
        gate = after(train_up, piece)

    low_gated = after(low_up, piece)
    part = lax.dynamic_slice(low_gated, (mine * quarter, 0), (quarter, rank)).T
    gain = (norm_train + norm_step).astype(jnp.bfloat16)
    pack = jnp.concatenate([part, gain[None, :]], axis=0)
    got = [pack] + [send_small(pack, k) for k in range(1, zero)]
    stack = jnp.stack(got)
    parts = [stack] + [send(stack, k, "model", model) for k in range(1, model)]
    grid = jnp.stack(parts)
    from_zero = jnp.stack([source_of(me, zero, k) for k in range(zero)])
    from_model = jnp.stack([source_of(mine, model, k) for k in range(model)])
    back_zero = jnp.argsort(from_zero) if zero & (zero - 1) else from_zero
    back_model = jnp.argsort(from_model) if model & (model - 1) else from_model
    grid = grid[back_model][:, back_zero]
    low_all = grid[:, :, :rank, :].transpose(1, 0, 3, 2).reshape(total_rows, rank)
    serve_norm = grid[:, :, rank, :].transpose(1, 0, 2).reshape(total_rows)

    gate = after(train_up, pack)
    whole = gate.astype(jnp.float32) + mix_rate * jnp.dot(
        low_up, high_up, preferred_element_type=jnp.float32
    )
    sums = jnp.sum(jnp.abs(whole), axis=0).reshape(zero, width)
    total = lax.dynamic_index_in_dim(sums, me, 0, keepdims=False)
    gate = train_up
    for k in range(1, zero):
        slice_sum = lax.dynamic_index_in_dim(sums, target_of(me, zero, k), 0, keepdims=False)
        gate = after(gate, slice_sum)
        total = total + send_small(slice_sum, k)
    scale_up = total / total_rows

    for k in order[1:]:
        for start, count in pieces[k]:
            piece = cut(gate, k, start, count)
            blocks[k, start] = send_block(piece, k)
            gate = after(train_up, piece)

    high = lax.dynamic_slice(high_up, (0, me * width), (rank, width))
    inverse = (total_rows / total)[None, :]
    zero_column = jnp.int32(0)
    out = merge_block(None, total_rows, train_up, low_all, high, inverse, me, me, rows, 0)
    for k in far[:-1] + near + far[-1:]:
        for start, count in pieces[k]:
            out = merge_block(
                out, total_rows, blocks[k, start], low_all, high, inverse, source_of(me, zero, k), zero_column, rows, start
            )
    return out, scale_up, serve_norm


def solution(mesh):
    zero, model = mesh.shape["zero"], mesh.shape["model"]
    in_specs = (
        P("zero", "model"),
        P("zero", None),
        P(None, "model"),
        P(("zero", "model")),
        P(("zero", "model")),
    )
    out_specs = (P(None, ("model", "zero")), P(("model", "zero")), P())

    def whole(train_up, *others):
        step = jax.shard_map(
            functools.partial(local, zero, model), mesh=mesh, in_specs=in_specs, out_specs=out_specs, check_vma=False
        )
        return step(train_up, *others)

    return whole
```

time: 1000 us -> 935 us (0.935)
  the two profiles are of different devices: /device:TPU:17 before, /device:TPU:28 now
where the time goes in v1:
time: 935 us; the launch traced here: 934 us
  waiting for transfers between devices  652 us (70%)
  starting transfers between devices  139 us (15%)
  Pallas kernels  70.2 us (8%)
  local copies, waits for them, and re-layouts  50.2 us (5%)
  matrix products  18 us (2%)
    ppermute x27, waiting for transfers between devices, send(): return lax.ppermute(value, axis, partner_pairs(size, k))  652 us
    ppermute x27, starting transfers between devices, send(): return lax.ppermute(value, axis, partner_pairs(size, k))  139 us
    pallas_call x11, Pallas kernels, merge_block(): pl.pallas_call(merge_body, grid_spec=pltpu.PrefetchScalarGridSpec(num_sca...  70.2 us
    dynamic_slice x10, local copies, waits for them, and re-layouts, cut(): lax.dynamic_slice(source, (start, target_of(me, zero, k) * width), (count...  38.1 us
  transfers between devices with their start and end apart: 27, of which 11 were waited for; matrix products, arithmetic and copies ran while one was open for 7% of the time, Pallas kernels for 7%

profile of v1, /device:TPU:28, one launch (start us, length us, event | category | flops | bytes accessed | tf_op | source)
XLA Modules:
  0.0 933.6 jit_solution(8995796314598057118)
XLA Ops:
  0.7 1.4 constant_dynamic-slice_fusion.7
  2.1 4.1 constant_dynamic-slice_fusion.10
  6.3 1.6 collective-permute-start.1
  7.8 0.4 collective-permute-start.2
  8.3 0.3 collective-permute-start.25
  8.6 18.0 %abs_reduce_fusion = f32[12288]{0:T(1024)S(1)} fusion(bf16[1536,12288]{1,0:T(8,128)(2,1)} %block_ref.1, bf16[1536,32]{0,1:T(8,128)(2,1)S(1)} %copy-done.6, bf16[32,12288]{1,0:T(8,128)(2,1)S(1)} %copy-done), kind=kOutput, calls=%fused_computation.2 | convolution fusion | flops 1302319104 | bytes 38682624 | tf_op jit(solution)/shard_map/dot_general | solution.py:149
  26.7 0.7 dynamic-slice_reduce_fusion
  27.4 0.5 collective-permute-start.11
  27.9 1.7 collective-permute-start.12
  29.6 4.8 constant_dynamic-slice_fusion.6
  34.4 1.3 collective-permute-start.3
  35.7 4.9 constant_dynamic-slice_fusion.5
  40.5 44.4 %collective-permute-done.12 = f32[1536]{0:T(1024)S(1)} collective-permute-done((f32[1536]{0:T(1024)S(1)}, f32[1536]{0:T(1024)S(1)}, u32[]{:S(2)}, u32[]{:S(2)}) %collective-permute-start.12) | collective-permute-done | bytes 6176 | tf_op jit(solution)/shard_map/ppermute | solution.py:109
  84.9 4.3 collective-permute-start.4
  89.2 1.9 collective-permute-start.6
  91.1 2.8 collective-permute-start.7
  93.9 3.2 constant_dynamic-slice_fusion.4
  97.2 70.0 %collective-permute-done.4 = bf16[33,384]{1,0:T(8,128)(2,1)S(1)} collective-permute-done((bf16[33,384]{1,0:T(8,128)(2,1)S(1)}, bf16[33,384]{1,0:T(8,128)(2,1)S(1)}, u32[]{:S(2)}, u32[]{:S(2)}) %collective-permute-start.4) | collective-permute-done | bytes 25376 | tf_op jit(solution)/shard_map/ppermute | solution.py:109
  167.5 0.9 collective-permute-start.14
  168.4 3.0 collective-permute-start.15
  171.4 0.8 collective-permute-start.24
  172.2 2.4 constant_dynamic-slice_fusion.9
  175.0 1.9 stack.149
  176.9 3.3 collective-permute-start.16
  180.2 1.6 collective-permute-start.17
  181.7 2.4 constant_dynamic-slice_fusion.8
  184.1 90.8 %collective-permute-done.16 = f32[1536]{0:T(1024)S(1)} collective-permute-done((f32[1536]{0:T(1024)S(1)}, f32[1536]{0:T(1024)S(1)}, u32[]{:S(2)}, u32[]{:S(2)}) %collective-permute-start.16) | collective-permute-done | bytes 6176 | tf_op jit(solution)/shard_map/ppermute | solution.py:109
  274.9 101.8 %collective-permute-start.26 = (bf16[384,1536]{1,0:T(8,128)(2,1)S(1)}, bf16[384,1536]{1,0:T(8,128)(2,1)S(1)}, u32[]{:S(2)}, u32[]{:S(2)}) collective-permute-start(bf16[384,1536]{1,0:T(8,128)(2,1)S(1)} %constant_dynamic-slice_fusion.7), channel_id=1, source_target_pairs={{0,16},{4,20},{8,24},{12,28},{16,0},{20,4},{24,8},{28,12},{1,17},{... | collective-permute-start | bytes 3538952 | tf_op jit(solution)/shard_map/ppermute | solution.py:109
  376.7 0.5 collective-permute-start.9
  377.2 4.8 constant_dynamic-slice_fusion.2
  382.1 2.6 collective-permute-done.9
  384.7 1.8 collective-permute-start.23
  386.5 1.5 collective-permute-start.22
  388.1 4.8 constant_dynamic-slice_fusion.1
  392.9 136.8 %collective-permute-done.26.block_ref = bf16[384,1536]{1,0:T(8,128)(2,1)S(1)} collective-permute-done((bf16[384,1536]{1,0:T(8,128)(2,1)S(1)}, bf16[384,1536]{1,0:T(8,128)(2,1)S(1)}, u32[]{:S(2)}, u32[]{:S(2)}) %collective-permute-start.26) | collective-permute-done | bytes 1179680 | tf_op jit(solution)/shard_map/ppermute | solution.py:109
  529.7 5.3 constant_dynamic-slice_fusion
  535.0 2.8 collective-permute-start.20
  538.1 1.5 collective-permute-start.19
  540.2 3.3 collective-permute-start.18
  543.4 1.5 collective-permute-start
  545.0 0.6 broadcast_multiply_fusion
  545.6 1.3 pad_maximum_fusion
  546.9 0.7 gather_fusion
  547.9 1.3 gather_fusion.1
  549.3 1.2 slice_bitcast_fusion
  550.4 2.9 copy.120
  553.4 0.7 reshape.491
  554.1 8.5 shard_map.76.rest_0_
  562.6 2.0 shard_map.77.rest_0_
  564.6 6.7 shard_map.78.rest_0_
  571.4 8.4 shard_map.79.rest_0_
  579.7 8.4 shard_map.80.rest_0_
  588.1 8.4 shard_map.81.rest_0_
  596.4 38.3 %collective-permute-done.21.block_ref = bf16[1536,1536]{1,0:T(8,128)(2,1)} collective-permute-done((bf16[1536,1536]{1,0:T(8,128)(2,1)}, bf16[1536,1536]{1,0:T(8,128)(2,1)}, u32[]{:S(2)}, u32[]{:S(2)}) %collective-permute-start.21) | collective-permute-done | bytes 4718624 | tf_op jit(solution)/shard_map/ppermute | solution.py:109
  634.7 8.4 shard_map.82.rest_0_
  643.1 182.8 %collective-permute-done.20.block_ref = bf16[1536,1536]{1,0:T(8,128)(2,1)} collective-permute-done((bf16[1536,1536]{1,0:T(8,128)(2,1)}, bf16[1536,1536]{1,0:T(8,128)(2,1)}, u32[]{:S(2)}, u32[]{:S(2)}) %collective-permute-start.20) | collective-permute-done | bytes 4718624 | tf_op jit(solution)/shard_map/ppermute | solution.py:109
  825.8 8.4 shard_map.83.rest_0_
  834.2 47.2 %collective-permute-done.19.block_ref = bf16[768,1536]{1,0:T(8,128)(2,1)} collective-permute-done((bf16[768,1536]{1,0:T(8,128)(2,1)}, bf16[768,1536]{1,0:T(8,128)(2,1)}, u32[]{:S(2)}, u32[]{:S(2)}) %collective-permute-start.19) | collective-permute-done | bytes 2359328 | tf_op jit(solution)/shard_map/ppermute | solution.py:109
  881.3 5.0 shard_map.84.rest_0_
  886.3 20.3 %collective-permute-done.18.block_ref = bf16[384,1536]{1,0:T(8,128)(2,1)} collective-permute-done((bf16[384,1536]{1,0:T(8,128)(2,1)}, bf16[384,1536]{1,0:T(8,128)(2,1)}, u32[]{:S(2)}, u32[]{:S(2)}) %collective-permute-start.18) | collective-permute-done | bytes 1179680 | tf_op jit(solution)/shard_map/ppermute | solution.py:109
  906.6 3.1 shard_map.85.rest_0_
  909.7 18.9 %collective-permute-done.block_ref = bf16[384,1536]{1,0:T(8,128)(2,1)} collective-permute-done((bf16[384,1536]{1,0:T(8,128)(2,1)}, bf16[384,1536]{1,0:T(8,128)(2,1)}, u32[]{:S(2)}, u32[]{:S(2)}) %collective-permute-start) | collective-permute-done | bytes 1179680 | tf_op jit(solution)/shard_map/ppermute | solution.py:109
  928.6 1.9 copy-done.3
  930.5 3.1 shard_map.86
  (72 shorter events, 1.9 us)
Async XLA Ops:
  0.6 8.0 copy-start
  0.7 5.5 copy-start.7
  0.7 5.5 copy-start.8
  0.7 5.5 copy-start.6
  6.3 83.0 %collective-permute-start.1 = (bf16[33,384]{1,0:T(8,128)(2,1)S(1)}, bf16[33,384]{1,0:T(8,128)(2,1)S(1)}, u32[]{:S(2)}, u32[]{:S(2)}) collective-permute-start(bf16[33,384]{1,0:T(8,128)(2,1)S(1)} %get-tuple-element.48), channel_id=1, source_target_pairs={{0,4},{4,0},{8,12},{12,8},{16,20},{20,16},{24,28},{28,24},{1,5},{5... | collective-permute-start | bytes 76040 | tf_op jit(solution)/shard_map/ppermute | solution.py:109
  7.8 81.4 %collective-permute-start.2 = (bf16[33,384]{1,0:T(8,128)(2,1)S(1)}, bf16[33,384]{1,0:T(8,128)(2,1)S(1)}, u32[]{:S(2)}, u32[]{:S(2)}) collective-permute-start(bf16[33,384]{1,0:T(8,128)(2,1)S(1)} %get-tuple-element.48), channel_id=1, source_target_pairs={{0,8},{4,12},{8,0},{12,4},{16,24},{20,28},{24,16},{28,20},{1,9},{5... | collective-permute-start | bytes 76040 | tf_op jit(solution)/shard_map/ppermute | solution.py:109
  8.3 526.7 %collective-permute-start.25 = (bf16[1152,1536]{1,0:T(8,128)(2,1)}, bf16[1152,1536]{1,0:T(8,128)(2,1)}, u32[]{:S(2)}, u32[]{:S(2)}) collective-permute-start(bf16[1152,1536]{1,0:T(8,128)(2,1)} %constant_dynamic-slice_fusion.10), channel_id=1, source_target_pairs={{0,16},{4,20},{8,24},{12,28},{16,0},{20,4},{24,8},{28,12},{1,17},{... | collective-permute-start | bytes 10616840 | tf_op jit(solution)/shard_map/ppermute | solution.py:109
  27.4 7.0 collective-permute-start.11
  27.9 57.0 %collective-permute-start.12 = (f32[1536]{0:T(1024)S(1)}, f32[1536]{0:T(1024)S(1)}, u32[]{:S(2)}, u32[]{:S(2)}) collective-permute-start(f32[1536]{0:T(1024)S(1)} %get-tuple-element.43), channel_id=1, source_target_pairs={{0,8},{4,12},{8,0},{12,4},{16,24},{20,28},{24,16},{28,20},{1,9},{5... | collective-permute-start | bytes 18440 | tf_op jit(solution)/shard_map/ppermute | solution.py:109
  34.4 56.7 %collective-permute-start.3 = (bf16[33,384]{1,0:T(8,128)(2,1)S(1)}, bf16[33,384]{1,0:T(8,128)(2,1)S(1)}, u32[]{:S(2)}, u32[]{:S(2)}) collective-permute-start(bf16[33,384]{1,0:T(8,128)(2,1)S(1)} %get-tuple-element.48), channel_id=1, source_target_pairs={{0,12},{4,8},{8,4},{12,0},{16,28},{20,24},{24,20},{28,16},{1,13},{... | collective-permute-start | bytes 76040 | tf_op jit(solution)/shard_map/ppermute | solution.py:109
  84.9 82.2 %collective-permute-start.4 = (bf16[33,384]{1,0:T(8,128)(2,1)S(1)}, bf16[33,384]{1,0:T(8,128)(2,1)S(1)}, u32[]{:S(2)}, u32[]{:S(2)}) collective-permute-start(bf16[33,384]{1,0:T(8,128)(2,1)S(1)} %get-tuple-element.48), channel_id=1, source_target_pairs={{0,16},{4,20},{8,24},{12,28},{16,0},{20,4},{24,8},{28,12},{1,17},{... | collective-permute-start | bytes 76040 | tf_op jit(solution)/shard_map/ppermute | solution.py:109
  89.2 78.3 %collective-permute-start.5 = (bf16[33,384]{1,0:T(8,128)(2,1)S(1)}, bf16[33,384]{1,0:T(8,128)(2,1)S(1)}, u32[]{:S(2)}, u32[]{:S(2)}) collective-permute-start(bf16[33,384]{1,0:T(8,128)(2,1)S(1)} %get-tuple-element.48), channel_id=1, source_target_pairs={{0,20},{4,16},{8,28},{12,24},{16,4},{20,0},{24,12},{28,8},{1,21},{... | collective-permute-start | bytes 76040 | tf_op jit(solution)/shard_map/ppermute | solution.py:109
  89.2 79.2 %collective-permute-start.6 = (bf16[33,384]{1,0:T(8,128)(2,1)S(1)}, bf16[33,384]{1,0:T(8,128)(2,1)S(1)}, u32[]{:S(2)}, u32[]{:S(2)}) collective-permute-start(bf16[33,384]{1,0:T(8,128)(2,1)S(1)} %get-tuple-element.48), channel_id=1, source_target_pairs={{0,24},{4,28},{8,16},{12,20},{16,8},{20,12},{24,0},{28,4},{1,25},{... | collective-permute-start | bytes 76040 | tf_op jit(solution)/shard_map/ppermute | solution.py:109
  91.1 80.2 %collective-permute-start.7 = (bf16[33,384]{1,0:T(8,128)(2,1)S(1)}, bf16[33,384]{1,0:T(8,128)(2,1)S(1)}, u32[]{:S(2)}, u32[]{:S(2)}) collective-permute-start(bf16[33,384]{1,0:T(8,128)(2,1)S(1)} %get-tuple-element.48), channel_id=1, source_target_pairs={{0,28},{4,24},{8,20},{12,16},{16,12},{20,8},{24,4},{28,0},{1,29},{... | collective-permute-start | bytes 76040 | tf_op jit(solution)/shard_map/ppermute | solution.py:109
  167.2 9.7 %collective-permute-start.13 = (f32[1536]{0:T(1024)S(1)}, f32[1536]{0:T(1024)S(1)}, u32[]{:S(2)}, u32[]{:S(2)}) collective-permute-start(f32[1536]{0:T(1024)S(1)} %get-tuple-element.42), channel_id=1, source_target_pairs={{0,12},{4,8},{8,4},{12,0},{16,28},{20,24},{24,20},{28,16},{1,13},{... | collective-permute-start | bytes 18440 | tf_op jit(solution)/shard_map/ppermute | solution.py:109
  167.5 12.7 %collective-permute-start.14 = (f32[1536]{0:T(1024)S(1)}, f32[1536]{0:T(1024)S(1)}, u32[]{:S(2)}, u32[]{:S(2)}) collective-permute-start(f32[1536]{0:T(1024)S(1)} %get-tuple-element.41), channel_id=1, source_target_pairs={{0,16},{4,20},{8,24},{12,28},{16,0},{20,4},{24,8},{28,12},{1,17},{... | collective-permute-start | bytes 18440 | tf_op jit(solution)/shard_map/ppermute | solution.py:109
  168.4 13.3 %collective-permute-start.15 = (f32[1536]{0:T(1024)S(1)}, f32[1536]{0:T(1024)S(1)}, u32[]{:S(2)}, u32[]{:S(2)}) collective-permute-start(f32[1536]{0:T(1024)S(1)} %get-tuple-element.40), channel_id=1, source_target_pairs={{0,20},{4,16},{8,28},{12,24},{16,4},{20,0},{24,12},{28,8},{1,21},{... | collective-permute-start | bytes 18440 | tf_op jit(solution)/shard_map/ppermute | solution.py:109
  171.4 366.7 %collective-permute-start.24 = (bf16[1536,1536]{1,0:T(8,128)(2,1)}, bf16[1536,1536]{1,0:T(8,128)(2,1)}, u32[]{:S(2)}, u32[]{:S(2)}) collective-permute-start(bf16[1536,1536]{1,0:T(8,128)(2,1)} %constant_dynamic-slice_fusion.6), channel_id=1, source_target_pairs={{0,20},{4,16},{8,28},{12,24},{16,4},{20,0},{24,12},{28,8},{1,21},{... | collective-permute-start | bytes 14155784 | tf_op jit(solution)/shard_map/ppermute | solution.py:109
  176.9 98.0 %collective-permute-start.16 = (f32[1536]{0:T(1024)S(1)}, f32[1536]{0:T(1024)S(1)}, u32[]{:S(2)}, u32[]{:S(2)}) collective-permute-start(f32[1536]{0:T(1024)S(1)} %get-tuple-element.39), channel_id=1, source_target_pairs={{0,24},{4,28},{8,16},{12,20},{16,8},{20,12},{24,0},{28,4},{1,25},{... | collective-permute-start | bytes 18440 | tf_op jit(solution)/shard_map/ppermute | solution.py:109
  180.2 196.6 %collective-permute-start.17 = (f32[1536]{0:T(1024)}, f32[1536]{0:T(1024)S(1)}, u32[]{:S(2)}, u32[]{:S(2)}) collective-permute-start(f32[1536]{0:T(1024)} %get-tuple-element.38), channel_id=1, source_target_pairs={{0,28},{4,24},{8,20},{12,16},{16,12},{20,8},{24,4},{28,0},{1,29},{... | collective-permute-start | bytes 18440 | tf_op jit(solution)/shard_map/ppermute | solution.py:109
  181.7 195.5 %collective-permute-start.8 = (bf16[8,33,384]{2,0,1:T(8,128)(2,1)S(1)}, bf16[8,33,384]{2,0,1:T(8,128)(2,1)}, u32[]{:S(2)}, u32[]{:S(2)}) collective-permute-start(bf16[8,33,384]{2,0,1:T(8,128)(2,1)S(1)} %stack.149), channel_id=1, source_target_pairs={{0,1},{1,0},{2,3},{3,2},{4,5},{5,4},{6,7},{7,6},{8,9},{9,8},{10,11... | collective-permute-start | bytes 608264 | tf_op jit(solution)/shard_map/ppermute | solution.py:109
  274.9 254.8 %collective-permute-start.26 = (bf16[384,1536]{1,0:T(8,128)(2,1)S(1)}, bf16[384,1536]{1,0:T(8,128)(2,1)S(1)}, u32[]{:S(2)}, u32[]{:S(2)}) collective-permute-start(bf16[384,1536]{1,0:T(8,128)(2,1)S(1)} %constant_dynamic-slice_fusion.7), channel_id=1, source_target_pairs={{0,16},{4,20},{8,24},{12,28},{16,0},{20,4},{24,8},{28,12},{1,17},{... | collective-permute-start | bytes 3538952 | tf_op jit(solution)/shard_map/ppermute | solution.py:109
  376.7 8.0 collective-permute-start.9
  377.2 9.3 collective-permute-start.10
  384.7 155.5 %collective-permute-start.23 = (bf16[1536,1536]{1,0:T(8,128)(2,1)}, bf16[1536,1536]{1,0:T(8,128)(2,1)}, u32[]{:S(2)}, u32[]{:S(2)}) collective-permute-start(bf16[1536,1536]{1,0:T(8,128)(2,1)} %constant_dynamic-slice_fusion.5), channel_id=1, source_target_pairs={{0,24},{4,28},{8,16},{12,20},{16,8},{20,12},{24,0},{28,4},{1,25},{... | collective-permute-start | bytes 14155784 | tf_op jit(solution)/shard_map/ppermute | solution.py:109
  386.5 156.9 %collective-permute-start.22 = (bf16[1536,1536]{1,0:T(8,128)(2,1)}, bf16[1536,1536]{1,0:T(8,128)(2,1)}, u32[]{:S(2)}, u32[]{:S(2)}) collective-permute-start(bf16[1536,1536]{1,0:T(8,128)(2,1)} %constant_dynamic-slice_fusion.2), channel_id=1, source_target_pairs={{0,4},{4,0},{8,12},{12,8},{16,20},{20,16},{24,28},{28,24},{1,5},{5... | collective-permute-start | bytes 14155784 | tf_op jit(solution)/shard_map/ppermute | solution.py:109
  529.7 5.3 copy-start.4
  529.7 105.0 %collective-permute-start.21 = (bf16[1536,1536]{1,0:T(8,128)(2,1)}, bf16[1536,1536]{1,0:T(8,128)(2,1)}, u32[]{:S(2)}, u32[]{:S(2)}) collective-permute-start(bf16[1536,1536]{1,0:T(8,128)(2,1)} %constant_dynamic-slice_fusion.1), channel_id=1, source_target_pairs={{0,8},{4,12},{8,0},{12,4},{16,24},{20,28},{24,16},{28,20},{1,9},{5... | collective-permute-start | bytes 14155784 | tf_op jit(solution)/shard_map/ppermute | solution.py:109
  535.0 290.8 %collective-permute-start.20 = (bf16[1536,1536]{1,0:T(8,128)(2,1)}, bf16[1536,1536]{1,0:T(8,128)(2,1)}, u32[]{:S(2)}, u32[]{:S(2)}) collective-permute-start(bf16[1536,1536]{1,0:T(8,128)(2,1)} %constant_dynamic-slice_fusion), channel_id=1, source_target_pairs={{0,12},{4,8},{8,4},{12,0},{16,28},{20,24},{24,20},{28,16},{1,13},{... | collective-permute-start | bytes 14155784 | tf_op jit(solution)/shard_map/ppermute | solution.py:109
  538.1 343.3 %collective-permute-start.19 = (bf16[768,1536]{1,0:T(8,128)(2,1)}, bf16[768,1536]{1,0:T(8,128)(2,1)}, u32[]{:S(2)}, u32[]{:S(2)}) collective-permute-start(bf16[768,1536]{1,0:T(8,128)(2,1)} %constant_dynamic-slice_fusion.4), channel_id=1, source_target_pairs={{0,28},{4,24},{8,20},{12,16},{16,12},{20,8},{24,4},{28,0},{1,29},{... | collective-permute-start | bytes 7077896 | tf_op jit(solution)/shard_map/ppermute | solution.py:109
  540.2 366.4 %collective-permute-start.18 = (bf16[384,1536]{1,0:T(8,128)(2,1)}, bf16[384,1536]{1,0:T(8,128)(2,1)}, u32[]{:S(2)}, u32[]{:S(2)}) collective-permute-start(bf16[384,1536]{1,0:T(8,128)(2,1)} %constant_dynamic-slice_fusion.9), channel_id=1, source_target_pairs={{0,28},{4,24},{8,20},{12,16},{16,12},{20,8},{24,4},{28,0},{1,29},{... | collective-permute-start | bytes 3538952 | tf_op jit(solution)/shard_map/ppermute | solution.py:109
  543.4 385.2 %collective-permute-start = (bf16[384,1536]{1,0:T(8,128)(2,1)}, bf16[384,1536]{1,0:T(8,128)(2,1)}, u32[]{:S(2)}, u32[]{:S(2)}) collective-permute-start(bf16[384,1536]{1,0:T(8,128)(2,1)} %constant_dynamic-slice_fusion.8), channel_id=1, source_target_pairs={{0,28},{4,24},{8,20},{12,16},{16,12},{20,8},{24,4},{28,0},{1,29},{... | collective-permute-start | bytes 3538952 | tf_op jit(solution)/shard_map/ppermute | solution.py:109
  553.4 353.3 %copy-start.2 = (bf16[8,4,384,32]{3,2,1,0:T(8,128)(2,1)}, bf16[8,4,384,32]{3,2,1,0:T(8,128)(2,1)S(1)}, u32[]{:S(2)}) copy-start(bf16[8,4,384,32]{3,2,1,0:T(8,128)(2,1)S(1)} %copy.120) | copy-start | bytes 2359300
  554.1 8.5 copy-start.5
  928.6 1.9 copy-start.3
  930.5 3.1 copy-start.1
